TPU v7x, 32 devices: a whole 2x2x4 slice. The times are simulated.
32 devices in a mesh: py: 4 (over y, core), pz: 8 (over z, x).
Axes of the slice: x: 2, y: 2, z: 4, core: 2. Of those that a mesh axis runs over, the one named last changes fastest.
Arguments:
- wavefunctions: float32 [2, 8, 128, 128, 128], P(None, None, 'pz', 'py'), may hold values from -6 to 6
- potential: float32 [128, 128, 128], P('pz', 'py'), may hold values from -4 to 4
- cutoff_sq: int32 [1], replicated, may hold values from 2304 to 4096
- locked_mask: int32 [8], replicated, may hold values 0 or 1
Outputs:
- applied: float32 [2, 8, 128, 128, 128], P(None, None, 'pz', 'py')
- rayleigh: float32 [8], replicated
- residual_norm: float32 [8], replicated
All inputs are finite; a program needn't handle non-finite values.
Results may differ from a plain program's by a relative error of at most 0.00005.
Values sent between devices are 32-bit elements; how exact they have to be, the bound alone decides.
A program may use at most 64 MiB of HBM per device.

v0:
```python
import math
import jax
import jax.numpy as jnp
from jax import lax
from jax.sharding import PartitionSpec as P


def make_tables(length, inverse):
    counter = jnp.arange(length, dtype=jnp.int32)
    phase = counter[:, None] * counter[None, :] % length
    angle = 2.0 * math.pi / length * phase.astype(jnp.float32)
    if inverse:
        return (jnp.cos(angle) / length, jnp.sin(angle) / length)
    return (jnp.cos(angle), -jnp.sin(angle))


def transform_axis(field, axis, tables):
    cosines, sines = tables
    letters = "abcdefgh"[: field.ndim - 1]
    place = axis - 1
    source = letters[:place] + "n" + letters[place + 1 :]
    target = letters[:place] + "k" + letters[place + 1 :]
    form = source + ",kn->" + target
    real_part = field[0]
    imag_part = field[1]
    high = lax.Precision.HIGHEST
    out_real = jnp.einsum(form, real_part, cosines, precision=high) - jnp.einsum(
        form, imag_part, sines, precision=high
    )
    out_imag = jnp.einsum(form, real_part, sines, precision=high) + jnp.einsum(
        form, imag_part, cosines, precision=high
    )
    return jnp.stack([out_real, out_imag])


def signed_square(counter, length):
    signed = jnp.where(counter < length // 2, counter, counter - length)
    return signed * signed


def kinetic_table(first_sq, second_sq, third_sq, cutoff_sq, length):
    total = first_sq[:, None, None] + second_sq[None, :, None] + third_sq[None, None, :]
    keep = (total <= cutoff_sq[0]).astype(jnp.float32)
    return 0.5 * (math.pi / length) ** 2 * total.astype(jnp.float32) * keep


def slab_kinetic(field, cutoff_sq, forward, inverse):
    parts, bands, rows_z, rows_y, length = field.shape
    size_y = lax.axis_size("py")
    size_z = lax.axis_size("pz")
    along_x = transform_axis(field, 4, forward)
    flat = jnp.moveaxis(along_x, 1, 3).reshape(parts, rows_z, rows_y, bands * length)
    planes = lax.all_to_all(
        lax.all_to_all(flat, "py", split_axis=3, concat_axis=2, tiled=True),
        "pz",
        split_axis=3,
        concat_axis=1,
        tiled=True,
    )
    width = planes.shape[3]
    start = lax.axis_index("py") * (bands * length // size_y) + lax.axis_index("pz") * width
    column = start + jnp.arange(width, dtype=jnp.int32)
    full_counter = jnp.arange(length, dtype=jnp.int32)
    full_sq = signed_square(full_counter, length)
    kinetic = kinetic_table(
        full_sq, full_sq, signed_square(column % length, length), cutoff_sq, length
    )
    spectrum = transform_axis(transform_axis(planes, 1, forward), 2, forward) * kinetic
    spatial = transform_axis(transform_axis(spectrum, 2, inverse), 1, inverse)
    returned = lax.all_to_all(
        lax.all_to_all(spatial, "py", split_axis=2, concat_axis=3, tiled=True),
        "pz",
        split_axis=1,
        concat_axis=3,
        tiled=True,
    )
    ordered = returned.reshape(parts, rows_z, rows_y, size_z, size_y, width)
    ordered = jnp.swapaxes(ordered, 3, 4).reshape(parts, rows_z, rows_y, bands, length)
    return transform_axis(jnp.moveaxis(ordered, 3, 1), 4, inverse)


def apply_kinetic(field, cutoff_sq, forward, inverse):
    return slab_kinetic(field, cutoff_sq, forward, inverse)


def body(wavefunctions, potential, cutoff_sq, locked_mask):
    length = wavefunctions.shape[4]
    forward = make_tables(length, False)
    inverse = make_tables(length, True)
    blocks = wavefunctions.shape[1] // 4

    def one_block(block, result):
        piece = lax.dynamic_slice_in_dim(wavefunctions, block * 4, 4, 1)
        done = apply_kinetic(piece, cutoff_sq, forward, inverse)
        return lax.dynamic_update_slice_in_dim(result, done, block * 4, 1)

    kinetic_part = lax.fori_loop(0, blocks, one_block, jnp.zeros_like(wavefunctions))
    applied = kinetic_part + potential[None, None] * wavefunctions
    norm_local = jnp.sum(wavefunctions * wavefunctions, axis=(0, 2, 3, 4))
    correlation_local = jnp.sum(wavefunctions * applied, axis=(0, 2, 3, 4))
    norm_sq, correlation = lax.psum((norm_local, correlation_local), ("py", "pz"))
    rayleigh = correlation / norm_sq
    residual = applied - rayleigh[None, :, None, None, None] * wavefunctions
    residual_sq = lax.psum(jnp.sum(residual * residual, axis=(0, 2, 3, 4)), ("py", "pz"))
    residual_norm = jnp.sqrt(residual_sq / norm_sq) * (1.0 - locked_mask.astype(jnp.float32))
    return (applied, rayleigh, residual_norm)


def solution(mesh):
    in_specs = (P(None, None, "pz", "py", None), P("pz", "py", None), P(), P())
    out_specs = (P(None, None, "pz", "py", None), P(), P())
    return jax.shard_map(body, mesh=mesh, in_specs=in_specs, out_specs=out_specs, check_vma=False)
```

profile of v0, /device:TPU:0, one launch (start us, length us, event | category | flops | bytes accessed | tf_op | source)
XLA Modules:
  0.0 693.6 jit_solution(16688748125790381216)
XLA Ops:
  0.6 2.5 broadcast_in_dim.14
  3.2 599.9 %while.18 = (s32[]{:T(128)}, f32[2,8,16,32,128]{4,3,2,1,0:T(8,128)}, f32[2,8,16,32,128]{4,3,2,1,0:T(8,128)}, s32[1]{0:T(128)}, s32[]{:T(128)}, /*index=5*/s32[]{...) while((s32[]{:T(128)}, ...), condition=%wide.region_1.2_spmd.clone.clone, body=%wide.region_0.1_spmd.clone.clone.sunk | while | flops 9676570624 | bytes 232916592 | solution.py:97
  3.2 2.5 fusion.346
  5.7 2.4 fusion.344
  8.1 2.5 fusion.347
  10.6 2.5 fusion.345
  13.3 7.5 %copy.142 = f32[2,16,32,4,128]{2,1,0,4,3:T(8,128)} copy(f32[2,16,32,4,128]{4,2,1,3,0:T(8,128)S(1)} %maximum_bitcast_fusion.2) | data formatting | bytes 4194304 | tf_op jit(solution)/shard_map/while/body/eval_jaxpr/reshape | solution.py:52
  20.7 6.1 reshape.143
  26.9 30.2 %all_to_all.204 = f32[4,1,131072]{2,1,0:T(1,128)} all-to-all(f32[4,1,131072]{2,1,0:T(1,128)S(1)} %reshape.143), channel_id=1, replica_groups=mesh['py'=4,'pz'=8] {'py'}, dimensions={0} | all-to-all | bytes 4194304 | tf_op jit(solution)/shard_map/while/body/eval_jaxpr/all_to_all | solution.py:54
  57.6 7.7 %reduce.4 = f32[4,131072]{1,0:T(4,128)S(1)} reduce(f32[4,1,131072]{2,1,0:T(1,128)} %all_to_all.204, f32[]{:T(128)} %broadcast.656), dimensions={1}, to_apply=%all_to_all.178.reduce_sub_computation | reduce | bytes 4194308 | tf_op jit(solution)/shard_map/while/body/eval_jaxpr/all_to_all | solution.py:54
  65.3 6.1 reshape.144
  71.4 5.2 copy.143
  78.2 3.1 copy.145
  81.3 6.9 all-to-all-start.1
  89.3 46.3 %all-to-all-done.1 = f32[2,16,128,128]{2,1,0,3:T(8,128)S(1)} async-done(((f32[2,16,128,128]{2,1,0,3:T(8,128)}), f32[2,16,128,128]{2,1,0,3:T(8,128)S(1)}, u32[]{:S(2)}, u32[]{:S(2)}) %all-to-all-start.1) | async-done | bytes 2097184 | tf_op jit(solution)/shard_map/while/body/eval_jaxpr/all_to_all | solution.py:53
  139.7 2.2 fusion.349
  144.7 2.4 fusion.350
  152.2 2.1 fusion.354
  165.6 2.0 fusion.365
  167.5 1.9 fusion.367
  170.9 28.1 %all_to_all.205 = f32[2,128,128,16]{1,3,0,2:T(8,128)S(1)} all-to-all(f32[2,128,128,16]{1,3,0,2:T(8,128)S(1)} %copy.151), channel_id=1, replica_groups=mesh['py'=4,'pz'=8] {'py'}, dimensions={2} | all-to-all | bytes 4194304 | tf_op jit(solution)/shard_map/while/body/eval_jaxpr/all_to_all | solution.py:71
  199.3 4.5 copy.153
  203.8 7.2 %reshape.145 = f32[8,1,65536]{2,1,0:T(1,128)} reshape(f32[128,2,32,64]{3,2,1,0:T(8,128)} %bitcast.327) | data formatting | bytes 4194304 | tf_op jit(solution)/shard_map/while
  211.0 3.9 all-to-all-start.3
  214.9 48.0 %all-to-all-done.3 = f32[8,1,65536]{2,1,0:T(1,128)S(1)} async-done(((f32[8,1,65536]{2,1,0:T(1,128)}), f32[8,1,65536]{2,1,0:T(1,128)S(1)}, u32[]{:S(2)}, u32[]{:S(2)}) %all-to-all-start.3) | async-done | bytes 2097184 | tf_op jit(solution)/shard_map/while/body/eval_jaxpr/all_to_all | solution.py:70
  264.8 7.2 %reduce.5 = f32[8,65536]{1,0:T(8,128)S(1)} reduce(f32[8,1,65536]{2,1,0:T(1,128)} %copy-done, f32[]{:T(128)} %broadcast.657), dimensions={1}, to_apply=%all_to_all.189.reduce_sub_computation | reduce | bytes 4194308 | tf_op jit(solution)/shard_map/while/body/eval_jaxpr/all_to_all | solution.py:70
  272.0 3.6 reshape.146
  275.6 7.0 %copy.154 = f32[2,16,32,8,64]{2,4,3,1,0:T(8,128)} copy(f32[2,16,32,8,64]{4,2,0,1,3:T(8,128)} %bitcast.326) | data formatting | bytes 4194304 | tf_op jit(solution)/shard_map/while/body/eval_jaxpr/all_to_all | solution.py:70
  282.6 7.9 %copy.155 = f32[2,16,32,4,8,16]{2,5,4,3,1,0:T(8,128)} copy(f32[2,16,32,4,8,16]{2,5,3,4,1,0:T(8,128)} %bitcast.320) | data formatting | bytes 4194304 | tf_op jit(solution)/shard_map/while/body/eval_jaxpr/transpose | solution.py:78
  290.5 5.6 copy.156
  301.3 2.0 copy-done.3
  303.5 2.4 fusion.346
  305.9 2.5 fusion.344
  308.4 2.5 fusion.347
  310.9 2.5 fusion.345
  313.5 7.5 %copy.142 = f32[2,16,32,4,128]{2,1,0,4,3:T(8,128)} copy(f32[2,16,32,4,128]{4,2,1,3,0:T(8,128)S(1)} %maximum_bitcast_fusion.2) | data formatting | bytes 4194304 | tf_op jit(solution)/shard_map/while/body/eval_jaxpr/reshape | solution.py:52
  321.0 6.1 reshape.143
  327.2 29.1 %all_to_all.204 = f32[4,1,131072]{2,1,0:T(1,128)} all-to-all(f32[4,1,131072]{2,1,0:T(1,128)S(1)} %reshape.143), channel_id=1, replica_groups=mesh['py'=4,'pz'=8] {'py'}, dimensions={0} | all-to-all | bytes 4194304 | tf_op jit(solution)/shard_map/while/body/eval_jaxpr/all_to_all | solution.py:54
  356.8 7.7 %reduce.4 = f32[4,131072]{1,0:T(4,128)S(1)} reduce(f32[4,1,131072]{2,1,0:T(1,128)} %all_to_all.204, f32[]{:T(128)} %broadcast.656), dimensions={1}, to_apply=%all_to_all.178.reduce_sub_computation | reduce | bytes 4194308 | tf_op jit(solution)/shard_map/while/body/eval_jaxpr/all_to_all | solution.py:54
  364.5 6.1 reshape.144
  370.6 5.2 copy.143
  377.5 3.1 copy.145
  380.5 4.0 all-to-all-start.1
  385.6 46.7 %all-to-all-done.1 = f32[2,16,128,128]{2,1,0,3:T(8,128)S(1)} async-done(((f32[2,16,128,128]{2,1,0,3:T(8,128)}), f32[2,16,128,128]{2,1,0,3:T(8,128)S(1)}, u32[]{:S(2)}, u32[]{:S(2)}) %all-to-all-start.1) | async-done | bytes 2097184 | tf_op jit(solution)/shard_map/while/body/eval_jaxpr/all_to_all | solution.py:53
  436.4 2.2 fusion.349
  441.3 2.4 fusion.350
  448.9 2.1 fusion.354
  462.2 2.0 fusion.365
  464.2 1.9 fusion.367
  467.6 28.1 %all_to_all.205 = f32[2,128,128,16]{1,3,0,2:T(8,128)S(1)} all-to-all(f32[2,128,128,16]{1,3,0,2:T(8,128)S(1)} %copy.151), channel_id=1, replica_groups=mesh['py'=4,'pz'=8] {'py'}, dimensions={2} | all-to-all | bytes 4194304 | tf_op jit(solution)/shard_map/while/body/eval_jaxpr/all_to_all | solution.py:71
  496.0 4.5 copy.153
  500.5 7.2 %reshape.145 = f32[8,1,65536]{2,1,0:T(1,128)} reshape(f32[128,2,32,64]{3,2,1,0:T(8,128)} %bitcast.327) | data formatting | bytes 4194304 | tf_op jit(solution)/shard_map/while
  507.7 3.9 all-to-all-start.3
  511.6 48.0 %all-to-all-done.3 = f32[8,1,65536]{2,1,0:T(1,128)S(1)} async-done(((f32[8,1,65536]{2,1,0:T(1,128)}), f32[8,1,65536]{2,1,0:T(1,128)S(1)}, u32[]{:S(2)}, u32[]{:S(2)}) %all-to-all-start.3) | async-done | bytes 2097184 | tf_op jit(solution)/shard_map/while/body/eval_jaxpr/all_to_all | solution.py:70
  561.5 7.2 %reduce.5 = f32[8,65536]{1,0:T(8,128)S(1)} reduce(f32[8,1,65536]{2,1,0:T(1,128)} %copy-done, f32[]{:T(128)} %broadcast.657), dimensions={1}, to_apply=%all_to_all.189.reduce_sub_computation | reduce | bytes 4194308 | tf_op jit(solution)/shard_map/while/body/eval_jaxpr/all_to_all | solution.py:70
  568.7 3.6 reshape.146
  572.3 7.0 %copy.154 = f32[2,16,32,8,64]{2,4,3,1,0:T(8,128)} copy(f32[2,16,32,8,64]{4,2,0,1,3:T(8,128)} %bitcast.326) | data formatting | bytes 4194304 | tf_op jit(solution)/shard_map/while/body/eval_jaxpr/all_to_all | solution.py:70
  579.3 7.9 %copy.155 = f32[2,16,32,4,8,16]{2,5,4,3,1,0:T(8,128)} copy(f32[2,16,32,4,8,16]{2,5,3,4,1,0:T(8,128)} %bitcast.320) | data formatting | bytes 4194304 | tf_op jit(solution)/shard_map/while/body/eval_jaxpr/transpose | solution.py:78
  587.2 5.6 copy.156
  598.0 2.0 copy-done.3
  603.1 6.5 multiply_reduce_fusion.1
  609.6 37.5 %all-reduce = (f32[8]{0:T(128)S(1)}, f32[8]{0:T(128)S(1)}) all-reduce(f32[8]{0:T(128)S(1)} %get-tuple-element.349, f32[8]{0:T(128)S(1)} %get-tuple-element.348), channel_id=1, replica_groups=mesh['py'=4,'pz'=8] {'py','pz'}, use_global_device_ids=true, to_apply=%region_3.4 | all-reduce | flops 16 | bytes 128 | tf_op jit(solution)/shard_map/psum | solution.py:101
  647.2 4.2 multiply_reduce_fusion
  651.4 41.5 %psum.23 = f32[8]{0:T(128)S(1)} all-reduce(f32[8]{0:T(128)S(1)} %multiply_reduce_fusion), channel_id=1, replica_groups=mesh['py'=4,'pz'=8] {'py','pz'}, use_global_device_ids=true, to_apply=%region_7.8 | all-reduce | flops 8 | bytes 64 | tf_op jit(solution)/shard_map/psum | solution.py:104
  (90 shorter events, 70.7 us)
Async XLA Ops:
  3.2 599.9 %copy-start.4 = (f32[16,32,128]{2,1,0:T(8,128)S(1)}, f32[16,32,128]{2,1,0:T(8,128)}, u32[]{:S(2)}) copy-start(f32[16,32,128]{2,1,0:T(8,128)} %param.7) | copy-start | bytes 786436
  81.3 54.2 %all-to-all-start.1 = ((f32[2,16,128,128]{2,1,0,3:T(8,128)}), f32[2,16,128,128]{2,1,0,3:T(8,128)S(1)}, u32[]{:S(2)}, u32[]{:S(2)}) async-start(f32[2,16,128,128]{2,1,0,3:T(8,128)} %copy.145), calls=%async_computation.1 | async-start | bytes 4194304 | tf_op jit(solution)/shard_map/while/body/eval_jaxpr/all_to_all | solution.py:53
  138.5 3.5 copy-start.1
  211.0 51.9 %all-to-all-start.3 = ((f32[8,1,65536]{2,1,0:T(1,128)}), f32[8,1,65536]{2,1,0:T(1,128)S(1)}, u32[]{:S(2)}, u32[]{:S(2)}) async-start(f32[8,1,65536]{2,1,0:T(1,128)} %reshape.145), calls=%async_computation.3 | async-start | bytes 4194304 | tf_op jit(solution)/shard_map/while/body/eval_jaxpr/all_to_all | solution.py:70
  262.9 1.4 copy-start
  298.6 2.5 copy-start.2
  301.3 2.0 copy-start.3
  380.5 51.7 %all-to-all-start.1 = ((f32[2,16,128,128]{2,1,0,3:T(8,128)}), f32[2,16,128,128]{2,1,0,3:T(8,128)S(1)}, u32[]{:S(2)}, u32[]{:S(2)}) async-start(f32[2,16,128,128]{2,1,0,3:T(8,128)} %copy.145), calls=%async_computation.1 | async-start | bytes 4194304 | tf_op jit(solution)/shard_map/while/body/eval_jaxpr/all_to_all | solution.py:53
  435.2 3.5 copy-start.1
  507.7 51.9 %all-to-all-start.3 = ((f32[8,1,65536]{2,1,0:T(1,128)}), f32[8,1,65536]{2,1,0:T(1,128)S(1)}, u32[]{:S(2)}, u32[]{:S(2)}) async-start(f32[8,1,65536]{2,1,0:T(1,128)} %reshape.145), calls=%async_computation.3 | async-start | bytes 4194304 | tf_op jit(solution)/shard_map/while/body/eval_jaxpr/all_to_all | solution.py:70
  559.6 1.4 copy-start
  595.2 2.5 copy-start.2
  598.0 2.0 copy-start.3
  647.1 4.2 copy-start.5
  647.2 45.7 %copy-start.6 = (s32[8]{0:T(128)S(1)}, s32[8]{0:T(128)}, u32[]{:S(2)}) copy-start(s32[8]{0:T(128)} %param.9) | copy-start | bytes 100
where the time goes:
time: 697 us; the launch traced here: 694 us
  blocking collectives  195 us (28%)
  waiting for transfers between devices  189 us (27%)
  local copies, waits for them, and re-layouts  156 us (22%)
  matrix products  85.4 us (12%)
  other arithmetic  44.8 us (6%)
  starting transfers between devices  18.7 us (3%)
    all_to_all x2, waiting for transfers between devices, slab_kinetic(): lax.all_to_all(lax.all_to_all(spatial, 'py', split_axis=2, concat_axis=3,...  96 us
    all_to_all x2, waiting for transfers between devices, slab_kinetic(): lax.all_to_all(lax.all_to_all(flat, 'py', split_axis=3, concat_axis=2, ti...  92.9 us
    all_to_all x2, blocking collectives, slab_kinetic(): lax.all_to_all(flat, 'py', split_axis=3, concat_axis=2, tiled=True)  59.3 us
    all_to_all x2, blocking collectives, slab_kinetic(): lax.all_to_all(spatial, 'py', split_axis=2, concat_axis=3, tiled=True)  56.3 us
    while x24, local copies, waits for them, and re-layouts  52.9 us
    psum x1, blocking collectives, body(): lax.psum(jnp.sum(residual * residual, axis=(0, 2, 3, 4)), ('py', 'pz'))  41.5 us
    psum x1, blocking collectives, body(): lax.psum((norm_local, correlation_local), ('py', 'pz'))  37.5 us
    dot_general x12, matrix products, transform_axis(): jnp.einsum(form, imag_part, sines, precision=high)  22.5 us
  transfers between devices with their start and end apart: 4, of which 4 were waited for; matrix products, arithmetic and copies ran while one was open for 0% of the time, Pallas kernels for 0%

commit v1 on v0

--- a/solution.py
+++ b/solution.py
@@ -98,7 +98,7 @@
     applied = kinetic_part + potential[None, None] * wavefunctions
     norm_local = jnp.sum(wavefunctions * wavefunctions, axis=(0, 2, 3, 4))
     correlation_local = jnp.sum(wavefunctions * applied, axis=(0, 2, 3, 4))
-    norm_sq, correlation = lax.psum((norm_local, correlation_local), ("py", "pz"))
+    norm_sq, correlation = lax.psum(lax.psum((norm_local, correlation_local), "pz"), "py")
     rayleigh = correlation / norm_sq
     residual = applied - rayleigh[None, :, None, None, None] * wavefunctions
     residual_sq = lax.psum(jnp.sum(residual * residual, axis=(0, 2, 3, 4)), ("py", "pz"))

time: 697 us -> 680 us (0.976)
  blocking collectives: 195 us -> 178 us
    psum x1 -> x2, blocking collectives: 37.5 us -> 25.1 us  [the longest x1 19.4 us: body(): lax.psum((norm_local, correlation_local), 'pz')]
where the time goes in v1:
time: 680 us; the launch traced here: 676 us
  waiting for transfers between devices  189 us (28%)
  blocking collectives  178 us (26%)
  local copies, waits for them, and re-layouts  156 us (23%)
  matrix products  85.4 us (13%)
  other arithmetic  44.8 us (7%)
  starting transfers between devices  18.7 us (3%)
    all_to_all x2, waiting for transfers between devices, slab_kinetic(): lax.all_to_all(lax.all_to_all(spatial, 'py', split_axis=2, concat_axis=3,...  96 us
    all_to_all x2, waiting for transfers between devices, slab_kinetic(): lax.all_to_all(lax.all_to_all(flat, 'py', split_axis=3, concat_axis=2, ti...  92.9 us
    all_to_all x2, blocking collectives, slab_kinetic(): lax.all_to_all(flat, 'py', split_axis=3, concat_axis=2, tiled=True)  59.3 us
    all_to_all x2, blocking collectives, slab_kinetic(): lax.all_to_all(spatial, 'py', split_axis=2, concat_axis=3, tiled=True)  56.3 us
    while x24, local copies, waits for them, and re-layouts  52.9 us
    psum x1, blocking collectives, body(): lax.psum(jnp.sum(residual * residual, axis=(0, 2, 3, 4)), ('py', 'pz'))  36.9 us
    dot_general x12, matrix products, transform_axis(): jnp.einsum(form, imag_part, sines, precision=high)  22.5 us
    dot_general x12, matrix products, transform_axis(): jnp.einsum(form, real_part, cosines, precision=high)  22 us
  transfers between devices with their start and end apart: 4, of which 4 were waited for; matrix products, arithmetic and copies ran while one was open for 0% of the time, Pallas kernels for 0%

profile of v1, /device:TPU:0, one launch (start us, length us, event | category | flops | bytes accessed | tf_op | source)
XLA Modules:
  0.0 676.3 jit_solution(3179466376171270911)
XLA Ops:
  0.6 2.5 broadcast_in_dim.14
  3.2 599.6 %while.18 = (s32[]{:T(128)}, f32[2,8,16,32,128]{4,3,2,1,0:T(8,128)}, f32[2,8,16,32,128]{4,3,2,1,0:T(8,128)}, s32[1]{0:T(128)}, s32[]{:T(128)}, /*index=5*/s32[]{...) while((s32[]{:T(128)}, ...), condition=%wide.region_1.2_spmd.clone.clone, body=%wide.region_0.1_spmd.clone.clone.sunk | while | flops 9676570624 | bytes 232916592 | solution.py:97
  3.2 2.5 fusion.346
  5.7 2.4 fusion.344
  8.1 2.5 fusion.347
  10.6 2.5 fusion.345
  13.3 7.5 %copy.142 = f32[2,16,32,4,128]{2,1,0,4,3:T(8,128)} copy(f32[2,16,32,4,128]{4,2,1,3,0:T(8,128)S(1)} %maximum_bitcast_fusion.2) | data formatting | bytes 4194304 | tf_op jit(solution)/shard_map/while/body/eval_jaxpr/reshape | solution.py:52
  20.7 6.1 reshape.143
  26.9 30.2 %all_to_all.204 = f32[4,1,131072]{2,1,0:T(1,128)} all-to-all(f32[4,1,131072]{2,1,0:T(1,128)S(1)} %reshape.143), channel_id=1, replica_groups=mesh['py'=4,'pz'=8] {'py'}, dimensions={0} | all-to-all | bytes 4194304 | tf_op jit(solution)/shard_map/while/body/eval_jaxpr/all_to_all | solution.py:54
  57.6 7.7 %reduce.4 = f32[4,131072]{1,0:T(4,128)S(1)} reduce(f32[4,1,131072]{2,1,0:T(1,128)} %all_to_all.204, f32[]{:T(128)} %broadcast.656), dimensions={1}, to_apply=%all_to_all.178.reduce_sub_computation | reduce | bytes 4194308 | tf_op jit(solution)/shard_map/while/body/eval_jaxpr/all_to_all | solution.py:54
  65.3 6.1 reshape.144
  71.4 5.2 copy.143
  78.2 3.1 copy.145
  81.3 6.9 %all-to-all-start.1 = ((f32[2,16,128,128]{2,1,0,3:T(8,128)}), f32[2,16,128,128]{2,1,0,3:T(8,128)S(1)}, u32[]{:S(2)}, u32[]{:S(2)}) async-start(f32[2,16,128,128]{2,1,0,3:T(8,128)} %copy.145), calls=%async_computation.1 | async-start | bytes 4194304 | tf_op jit(solution)/shard_map/while/body/eval_jaxpr/all_to_all | solution.py:53
  89.3 46.3 %all-to-all-done.1 = f32[2,16,128,128]{2,1,0,3:T(8,128)S(1)} async-done(((f32[2,16,128,128]{2,1,0,3:T(8,128)}), f32[2,16,128,128]{2,1,0,3:T(8,128)S(1)}, u32[]{:S(2)}, u32[]{:S(2)}) %all-to-all-start.1) | async-done | bytes 2097184 | tf_op jit(solution)/shard_map/while/body/eval_jaxpr/all_to_all | solution.py:53
  139.7 2.2 fusion.349
  144.7 2.4 fusion.350
  152.2 2.1 fusion.354
  165.6 2.0 fusion.365
  170.9 28.1 %all_to_all.205 = f32[2,128,128,16]{1,3,0,2:T(8,128)S(1)} all-to-all(f32[2,128,128,16]{1,3,0,2:T(8,128)S(1)} %copy.151), channel_id=1, replica_groups=mesh['py'=4,'pz'=8] {'py'}, dimensions={2} | all-to-all | bytes 4194304 | tf_op jit(solution)/shard_map/while/body/eval_jaxpr/all_to_all | solution.py:71
  199.3 4.5 copy.153
  203.8 7.2 %reshape.145 = f32[8,1,65536]{2,1,0:T(1,128)} reshape(f32[128,2,32,64]{3,2,1,0:T(8,128)} %bitcast.327) | data formatting | bytes 4194304 | tf_op jit(solution)/shard_map/while
  211.0 3.9 all-to-all-start.3
  214.9 48.0 %all-to-all-done.3 = f32[8,1,65536]{2,1,0:T(1,128)S(1)} async-done(((f32[8,1,65536]{2,1,0:T(1,128)}), f32[8,1,65536]{2,1,0:T(1,128)S(1)}, u32[]{:S(2)}, u32[]{:S(2)}) %all-to-all-start.3) | async-done | bytes 2097184 | tf_op jit(solution)/shard_map/while/body/eval_jaxpr/all_to_all | solution.py:70
  264.8 7.2 %reduce.5 = f32[8,65536]{1,0:T(8,128)S(1)} reduce(f32[8,1,65536]{2,1,0:T(1,128)} %copy-done, f32[]{:T(128)} %broadcast.657), dimensions={1}, to_apply=%all_to_all.189.reduce_sub_computation | reduce | bytes 4194308 | tf_op jit(solution)/shard_map/while/body/eval_jaxpr/all_to_all | solution.py:70
  272.0 3.6 reshape.146
  275.6 7.0 %copy.154 = f32[2,16,32,8,64]{2,4,3,1,0:T(8,128)} copy(f32[2,16,32,8,64]{4,2,0,1,3:T(8,128)} %bitcast.326) | data formatting | bytes 4194304 | tf_op jit(solution)/shard_map/while/body/eval_jaxpr/all_to_all | solution.py:70
  282.6 7.9 %copy.155 = f32[2,16,32,4,8,16]{2,5,4,3,1,0:T(8,128)} copy(f32[2,16,32,4,8,16]{2,5,3,4,1,0:T(8,128)} %bitcast.320) | data formatting | bytes 4194304 | tf_op jit(solution)/shard_map/while/body/eval_jaxpr/transpose | solution.py:78
  290.5 5.6 copy.156
  301.3 2.0 copy-done.3
  303.5 2.4 fusion.346
  305.9 2.5 fusion.344
  308.4 2.5 fusion.347
  310.9 2.5 fusion.345
  313.5 7.5 %copy.142 = f32[2,16,32,4,128]{2,1,0,4,3:T(8,128)} copy(f32[2,16,32,4,128]{4,2,1,3,0:T(8,128)S(1)} %maximum_bitcast_fusion.2) | data formatting | bytes 4194304 | tf_op jit(solution)/shard_map/while/body/eval_jaxpr/reshape | solution.py:52
  321.0 6.1 reshape.143
  327.2 29.1 %all_to_all.204 = f32[4,1,131072]{2,1,0:T(1,128)} all-to-all(f32[4,1,131072]{2,1,0:T(1,128)S(1)} %reshape.143), channel_id=1, replica_groups=mesh['py'=4,'pz'=8] {'py'}, dimensions={0} | all-to-all | bytes 4194304 | tf_op jit(solution)/shard_map/while/body/eval_jaxpr/all_to_all | solution.py:54
  356.8 7.7 %reduce.4 = f32[4,131072]{1,0:T(4,128)S(1)} reduce(f32[4,1,131072]{2,1,0:T(1,128)} %all_to_all.204, f32[]{:T(128)} %broadcast.656), dimensions={1}, to_apply=%all_to_all.178.reduce_sub_computation | reduce | bytes 4194308 | tf_op jit(solution)/shard_map/while/body/eval_jaxpr/all_to_all | solution.py:54
  364.5 6.1 reshape.144
  370.6 5.2 copy.143
  377.5 3.1 copy.145
  380.5 4.0 all-to-all-start.1
  385.6 46.7 %all-to-all-done.1 = f32[2,16,128,128]{2,1,0,3:T(8,128)S(1)} async-done(((f32[2,16,128,128]{2,1,0,3:T(8,128)}), f32[2,16,128,128]{2,1,0,3:T(8,128)S(1)}, u32[]{:S(2)}, u32[]{:S(2)}) %all-to-all-start.1) | async-done | bytes 2097184 | tf_op jit(solution)/shard_map/while/body/eval_jaxpr/all_to_all | solution.py:53
  436.4 2.2 fusion.349
  441.3 2.4 fusion.350
  448.9 2.1 fusion.354
  462.2 2.0 fusion.365
  464.2 1.9 fusion.367
  467.6 28.1 %all_to_all.205 = f32[2,128,128,16]{1,3,0,2:T(8,128)S(1)} all-to-all(f32[2,128,128,16]{1,3,0,2:T(8,128)S(1)} %copy.151), channel_id=1, replica_groups=mesh['py'=4,'pz'=8] {'py'}, dimensions={2} | all-to-all | bytes 4194304 | tf_op jit(solution)/shard_map/while/body/eval_jaxpr/all_to_all | solution.py:71
  496.0 4.5 copy.153
  500.5 7.2 %reshape.145 = f32[8,1,65536]{2,1,0:T(1,128)} reshape(f32[128,2,32,64]{3,2,1,0:T(8,128)} %bitcast.327) | data formatting | bytes 4194304 | tf_op jit(solution)/shard_map/while
  507.7 3.9 all-to-all-start.3
  511.6 48.0 %all-to-all-done.3 = f32[8,1,65536]{2,1,0:T(1,128)S(1)} async-done(((f32[8,1,65536]{2,1,0:T(1,128)}), f32[8,1,65536]{2,1,0:T(1,128)S(1)}, u32[]{:S(2)}, u32[]{:S(2)}) %all-to-all-start.3) | async-done | bytes 2097184 | tf_op jit(solution)/shard_map/while/body/eval_jaxpr/all_to_all | solution.py:70
  561.5 7.2 %reduce.5 = f32[8,65536]{1,0:T(8,128)S(1)} reduce(f32[8,1,65536]{2,1,0:T(1,128)} %copy-done, f32[]{:T(128)} %broadcast.657), dimensions={1}, to_apply=%all_to_all.189.reduce_sub_computation | reduce | bytes 4194308 | tf_op jit(solution)/shard_map/while/body/eval_jaxpr/all_to_all | solution.py:70
  568.7 3.6 reshape.146
  572.3 7.0 %copy.154 = f32[2,16,32,8,64]{2,4,3,1,0:T(8,128)} copy(f32[2,16,32,8,64]{4,2,0,1,3:T(8,128)} %bitcast.326) | data formatting | bytes 4194304 | tf_op jit(solution)/shard_map/while/body/eval_jaxpr/all_to_all | solution.py:70
  579.3 7.9 %copy.155 = f32[2,16,32,4,8,16]{2,5,4,3,1,0:T(8,128)} copy(f32[2,16,32,4,8,16]{2,5,3,4,1,0:T(8,128)} %bitcast.320) | data formatting | bytes 4194304 | tf_op jit(solution)/shard_map/while/body/eval_jaxpr/transpose | solution.py:78
  587.2 5.6 copy.156
  598.0 2.0 copy-done.3
  602.8 6.5 multiply_reduce_fusion.1
  609.3 19.4 %all-reduce = (f32[8]{0:T(128)S(1)}, f32[8]{0:T(128)S(1)}) all-reduce(f32[8]{0:T(128)S(1)} %get-tuple-element.349, f32[8]{0:T(128)S(1)} %get-tuple-element.348), channel_id=1, replica_groups=mesh['py'=4,'pz'=8] {'pz'}, use_global_device_ids=true, to_apply=%region_3.4 | all-reduce | flops 16 | bytes 128 | tf_op jit(solution)/shard_map/psum | solution.py:101
  628.8 5.6 all-reduce.1
  634.4 4.2 multiply_reduce_fusion
  638.7 36.9 %psum.39 = f32[8]{0:T(128)S(1)} all-reduce(f32[8]{0:T(128)S(1)} %multiply_reduce_fusion), channel_id=1, replica_groups=mesh['py'=4,'pz'=8] {'py','pz'}, use_global_device_ids=true, to_apply=%region_9.10 | all-reduce | flops 8 | bytes 64 | tf_op jit(solution)/shard_map/psum | solution.py:104
  (91 shorter events, 72.6 us)
Async XLA Ops:
  3.2 599.6 %copy-start.4 = (f32[16,32,128]{2,1,0:T(8,128)S(1)}, f32[16,32,128]{2,1,0:T(8,128)}, u32[]{:S(2)}) copy-start(f32[16,32,128]{2,1,0:T(8,128)} %param.7) | copy-start | bytes 786436
  81.3 54.2 %all-to-all-start.1 = ((f32[2,16,128,128]{2,1,0,3:T(8,128)}), f32[2,16,128,128]{2,1,0,3:T(8,128)S(1)}, u32[]{:S(2)}, u32[]{:S(2)}) async-start(f32[2,16,128,128]{2,1,0,3:T(8,128)} %copy.145), calls=%async_computation.1 | async-start | bytes 4194304 | tf_op jit(solution)/shard_map/while/body/eval_jaxpr/all_to_all | solution.py:53
  138.5 3.5 copy-start.1
  211.0 51.9 %all-to-all-start.3 = ((f32[8,1,65536]{2,1,0:T(1,128)}), f32[8,1,65536]{2,1,0:T(1,128)S(1)}, u32[]{:S(2)}, u32[]{:S(2)}) async-start(f32[8,1,65536]{2,1,0:T(1,128)} %reshape.145), calls=%async_computation.3 | async-start | bytes 4194304 | tf_op jit(solution)/shard_map/while/body/eval_jaxpr/all_to_all | solution.py:70
  262.9 1.4 copy-start
  298.6 2.5 copy-start.2
  301.3 2.0 copy-start.3
  380.5 51.7 %all-to-all-start.1 = ((f32[2,16,128,128]{2,1,0,3:T(8,128)}), f32[2,16,128,128]{2,1,0,3:T(8,128)S(1)}, u32[]{:S(2)}, u32[]{:S(2)}) async-start(f32[2,16,128,128]{2,1,0,3:T(8,128)} %copy.145), calls=%async_computation.1 | async-start | bytes 4194304 | tf_op jit(solution)/shard_map/while/body/eval_jaxpr/all_to_all | solution.py:53
  435.2 3.5 copy-start.1
  507.7 51.9 %all-to-all-start.3 = ((f32[8,1,65536]{2,1,0:T(1,128)}), f32[8,1,65536]{2,1,0:T(1,128)S(1)}, u32[]{:S(2)}, u32[]{:S(2)}) async-start(f32[8,1,65536]{2,1,0:T(1,128)} %reshape.145), calls=%async_computation.3 | async-start | bytes 4194304 | tf_op jit(solution)/shard_map/while/body/eval_jaxpr/all_to_all | solution.py:70
  559.6 1.4 copy-start
  595.2 2.5 copy-start.2
  598.0 2.0 copy-start.3
  634.4 4.2 copy-start.5
  634.4 41.1 %copy-start.6 = (s32[8]{0:T(128)S(1)}, s32[8]{0:T(128)}, u32[]{:S(2)}) copy-start(s32[8]{0:T(128)} %param.9) | copy-start | bytes 100
